TPU v7x, 256 devices: a whole 4x4x8 slice. The times are simulated.
256 devices in a mesh: wide: 32 (over z_hi, y, core), shard: 8 (over z_lo, x).
Axes of the slice: x: 4, y: 4, z: 8 (z_hi: 4, z_lo: 2; z = z_hi * 2 + z_lo), core: 2. Of those that a mesh axis runs over, the one named last changes fastest.
Arguments:
- weights: bfloat16 [1024, 8192], P('shard'), may hold values from -6 to 6
- momentum: bfloat16 [32, 1024, 8192], P('wide', 'shard'), may hold values from -6 to 6
- grads: bfloat16 [2, 32, 1024, 8192], P(None, 'wide', 'shard'), may hold values from -6 to 6
- offsets: int32 [8, 64], P('shard'), may hold values from 0 to 96
- owners: int32 [8, 64], P('shard'), may hold values from 0 to 63, each once within a row
- exp_avg: float32 [8, 64, 32, 128], P('shard', 'wide'), may hold values from -7 to 7
- exp_sq: float32 [8, 64, 32, 128], P('shard', 'wide'), may hold values from 0.01 to 1
Outputs:
- new_weights: bfloat16 [1024, 8192], P('shard')
- new_momentum: bfloat16 [32, 1024, 8192], P('wide', 'shard')
- new_avg: float32 [8, 64, 32, 128], P('shard', 'wide')
- new_sq: float32 [8, 64, 32, 128], P('shard', 'wide')
- scales: float32 [2], replicated
Inputs may be any that keep to these rules, and one draw needn't show every extreme that they name: `offsets`: each block's band spans 32 consecutive transform rows. Each row of owners is a permutation of 0 to 63.
All inputs are finite; a program needn't handle non-finite values.
Results may differ from a plain program's by a relative error of at most 0.003.
Values may be sent and summed in bfloat16 or wider, within the bound.
A program may use at most 128 MiB of HBM per device.

v0:
```python
import functools
import jax
import jax.numpy as jnp
from jax import lax
from jax.sharding import Mesh
from jax.sharding import PartitionSpec as P

STEPS = 2
WIDE = ("wide_0", "wide_1", "wide_2")
SHARD = ("shard_0", "shard_1")
WIDE_SHARD = ("wide_0", "wide_1", "wide_2", "shard_0", "shard_1")
highest = lax.Precision.HIGHEST
momentum_decay = 0.9
beta_one = 0.8
beta_two = 0.95
adam_eps = 1e-08
rms_eps = 1e-06
learning_rate = 0.2


def one_axis_at_a_time(shard, axes):
    return functools.reduce(lax.psum, axes, shard)


def laid_out(parts, dim):
    parts = jnp.moveaxis(parts, 0, dim)
    lengths = parts.shape
    return parts.reshape(*lengths[:dim], lengths[dim] * lengths[dim + 1], *lengths[dim + 2 :])


def from_everyone(shard, axis):
    length = lax.axis_size(axis)
    return lax.all_to_all(
        jnp.broadcast_to(shard[None], (length, *shard.shape)), axis, 0, 0, tiled=True
    )


def gathered_copies(shard, axis, dim):
    return laid_out(from_everyone(shard, axis), dim)


def dct_table(length):
    frequency = jnp.arange(length, dtype=jnp.float32)[:, None]
    position = jnp.arange(length, dtype=jnp.float32)[None, :]
    cosines = jnp.cos(jnp.pi * (2.0 * position + 1.0) * frequency / (2.0 * length))
    scaling = jnp.where(frequency == 0.0, jnp.sqrt(1.0 / length), jnp.sqrt(2.0 / length))
    return cosines * scaling


def band_tables(basis, offsets, band_rows):
    indices = offsets[:, :, None] + jnp.arange(band_rows, dtype=jnp.int32)[None, None, :]
    return basis[indices]


def inverse(coefs, picked, basis):
    right_part = jnp.einsum("rjpc,cb->rjpb", coefs, basis, precision=highest)
    return jnp.einsum("rjpa,rjpb->rajb", picked, right_part, precision=highest)


def per_device(weights, momentum, grads, offsets, owners, exp_avg, exp_sq):
    block_len = exp_avg.shape[3]
    band_rows = exp_avg.shape[2]
    basis = dct_table(block_len)
    picked = band_tables(basis, offsets, band_rows)
    slot_order = jnp.argsort(owners, axis=1)
    row_blocks = offsets.shape[0]
    col_blocks = offsets.shape[1]
    block_shape = (row_blocks, block_len, col_blocks, block_len)
    replicas = lax.axis_size(WIDE)
    count_all = exp_avg.size * lax.axis_size(WIDE) * lax.axis_size(SHARD)
    weight_now = weights.astype(jnp.float32).reshape(block_shape)
    moment_now = momentum[0].astype(jnp.float32).reshape(block_shape)
    avg_now = exp_avg
    sq_now = exp_sq
    scales = []
    for step_index in range(STEPS):
        blended = momentum_decay * moment_now + grads[step_index, 0].astype(jnp.float32).reshape(
            block_shape
        )
        left_part = jnp.einsum("rjpa,rajb->rjpb", picked, blended, precision=highest)
        band_coef = jnp.einsum("rjpb,cb->rjpc", left_part, basis, precision=highest)
        moment_now = blended - inverse(band_coef, picked, basis)
        slot_band = jnp.take_along_axis(band_coef, slot_order[:, :, None, None], axis=1)
        pieces = lax.all_to_all(
            slot_band.astype(jnp.bfloat16), WIDE, split_axis=1, concat_axis=0, tiled=True
        ).astype(slot_band.dtype)
        summed = jnp.sum(pieces.reshape((replicas, row_blocks) + pieces.shape[1:]), axis=0)
        mean_band = summed / replicas
        avg_now = beta_one * avg_now + (1.0 - beta_one) * mean_band
        sq_now = beta_two * sq_now + (1.0 - beta_two) * mean_band * mean_band
        raw_update = avg_now / (jnp.sqrt(sq_now) + adam_eps)
        power_sum = one_axis_at_a_time(jnp.sum(raw_update * raw_update), WIDE_SHARD)
        spread = jnp.sqrt(power_sum / count_all + rms_eps)
        update = (raw_update / spread).astype(jnp.bfloat16)
        gathered = gathered_copies(update, WIDE, 1)
        block_update = jnp.take_along_axis(
            gathered.astype(jnp.float32), owners[:, :, None, None], axis=1
        )
        weight_now = weight_now - learning_rate * inverse(block_update, picked, basis)
        scales.append(spread)
    new_weights = weight_now.reshape(weights.shape).astype(jnp.bfloat16)
    new_momentum = moment_now.reshape(momentum.shape).astype(jnp.bfloat16)
    return (new_weights, new_momentum, avg_now, sq_now, jnp.stack(scales))


def solution(mesh):
    split = Mesh(
        mesh.devices.reshape(4, 4, 2, 2, 4), ("wide_0", "wide_1", "wide_2", "shard_0", "shard_1")
    )
    in_specs = (
        P(SHARD, None),
        P(WIDE, SHARD, None),
        P(None, WIDE, SHARD, None),
        P(SHARD, None),
        P(SHARD, None),
        P(SHARD, WIDE, None, None),
        P(SHARD, WIDE, None, None),
    )
    out_specs = (
        P(SHARD, None),
        P(WIDE, SHARD, None),
        P(SHARD, WIDE, None, None),
        P(SHARD, WIDE, None, None),
        P(),
    )
    return jax.shard_map(
        per_device, mesh=split, in_specs=in_specs, out_specs=out_specs, check_vma=False
    )
```

profile of v0, /device:TPU:1, one launch (start us, length us, event | category | flops | bytes accessed | tf_op | source)
XLA Modules:
  0.0 243.5 jit_solution(2718648643845490075)
XLA Ops:
  0.6 0.7 copy.36
  1.4 1.0 sort.17
  2.6 0.7 compare_select_fusion
  3.4 6.6 %slice_convert_fusion.1 = (f32[1,1,128,8192]{3,2,1,0:T(8,128)}, f32[16,8,64,128]{3,1,2,0:T(8,128)S(1)}, f32[1,1,128,8192]{3,2,1,0:T(8,128)}) fusion(bf16[2,1,128,8192]{3,2,1,0:T(8,128)(2,1)} %param.11), kind=kLoop, calls=%fused_computation.20 | loop fusion | flops 2097152 | bytes 16777216 | tf_op jit(solution)/shard_map/convert_element_type | solution.py:77
  10.0 2.7 %copy.49 = f32[16,8,64,128]{3,2,1,0:T(8,128)} copy(f32[16,8,64,128]{3,1,2,0:T(8,128)S(1)} %get-tuple-element.42) | data formatting | bytes 8388608
  12.7 2.5 %convert_multiply_fusion = (f32[1,128,8192]{2,1,0:T(8,128)}, f32[16,8,64,128]{3,1,2,0:T(8,128)S(1)}) fusion(bf16[1,128,8192]{2,1,0:T(8,128)(2,1)S(1)} %copy-done.2), kind=kLoop, calls=%fused_computation.18 | loop fusion | flops 2097152 | bytes 10485760 | tf_op jit(solution)/shard_map/mul | solution.py:77
  15.3 2.7 %copy.48 = f32[16,8,64,128]{3,2,1,0:T(8,128)} copy(f32[16,8,64,128]{3,1,2,0:T(8,128)S(1)} %get-tuple-element.45) | data formatting | bytes 8388608
  17.9 0.2 cosine_multiply_fusion
  18.2 6.0 %gather_fusion = f32[2048,128]{1,0:T(8,128)S(1)} fusion(f32[128,128]{1,0:T(8,128)S(1)} %cosine_multiply_fusion, s32[2048]{0:T(1024)S(1)} %broadcast_clamp_fusion), kind=kCustom, calls=%fused_computation.4 | custom fusion | bytes 2105344 | tf_op jit(solution)/shard_map/gather | solution.py:52
  24.2 12.7 %fusion.6 = f32[64,32,128]{2,1,0:T(8,128)S(1)} fusion(f32[64,32,128]{2,1,0:T(8,128)S(1)} %bitcast.181, f32[128,64,128]{2,1,0:T(8,128)} %bitcast.188, f32[128,64,128]{2,1,0:T(8,128)} %bitcast.189), kind=kOutput, calls=%fused_computation.16 | convolution fusion | flops 403701760 | bytes 10485760 | tf_op jit(solution)/shard_map/rjpa,rajb->rjpb/dot_general | solution.py:80
  36.9 1.2 fusion.30
  38.1 1.2 fusion.27
  39.3 5.6 %copy.41 = f32[1,1,128,8192]{2,3,1,0:T(8,128)} copy(f32[1,1,128,8192]{3,2,1,0:T(8,128)} %get-tuple-element.41) | data formatting | bytes 8388608 | tf_op jit(solution)/shard_map/convert_element_type | solution.py:77
  44.9 5.6 %copy.42 = f32[1,1,128,8192]{2,3,1,0:T(8,128)} copy(f32[1,1,128,8192]{3,2,1,0:T(8,128)} %get-tuple-element.43) | data formatting | bytes 8388608 | tf_op jit(solution)/shard_map/convert_element_type | solution.py:77
  50.5 5.6 %copy.40 = f32[1,128,8192]{1,2,0:T(8,128)} copy(f32[1,128,8192]{2,1,0:T(8,128)} %get-tuple-element.44) | data formatting | bytes 8388608 | tf_op jit(solution)/shard_map/mul | solution.py:77
  56.1 10.1 %fusion.3 = f32[1,128,64,128]{1,3,2,0:T(8,128)S(1)} fusion(f32[1,128,64,128]{1,3,2,0:T(8,128)} %bitcast.191, f32[1,128,64,128]{1,3,2,0:T(8,128)} %bitcast.192, f32[1,128,64,128]{1,3,2,0:T(8,128)} %bitcast.190, f32[64,32,128]{2,1,0:T(8,128)S(1)} %fusion.27, f32[64,32,128]{2,1,0:T(8,128)S(1)} %bitcast.182), kind=kOutput, calls=%fused_computation.11 | convolution fusion | flops 406847488 | bytes 18874368 | tf_op jit(solution)/shard_map/rjpa,rjpb->rajb/dot_general | solution.py:57
  66.2 6.7 %fusion.4 = f32[64,32,128]{2,1,0:T(8,128)S(1)} fusion(f32[64,32,128]{2,1,0:T(8,128)S(1)} %bitcast.183, f32[1,128,64,128]{1,3,2,0:T(8,128)S(1)} %fusion.3), kind=kOutput, calls=%fused_computation.13 | convolution fusion | flops 402653184 | bytes 6291456 | tf_op jit(solution)/shard_map/rjpa,rajb->rjpb/dot_general | solution.py:80
  72.8 1.2 fusion.25
  74.1 1.4 gather_fusion.1
  75.6 0.7 gather_fusion.3
  76.2 2.1 fusion.17
  78.3 30.7 %all_to_all.28 = bf16[1,64,32,128]{3,2,0,1:T(8,128)(2,1)S(1)} all-to-all(bf16[1,64,32,128]{3,2,0,1:T(8,128)(2,1)S(1)} %get-tuple-element.47), channel_id=1, replica_groups=mesh['wide_0'=4,'wide_1'=4,'wide_2'=2,'shard_0'=2,'shard_1'=4] {'wide_0'..., dimensions={1} | all-to-all | bytes 1048576 | tf_op jit(solution)/shard_map/all_to_all | solution.py:84
  109.0 4.2 %all-to-all-start = ((bf16[1,64,32,128]{3,2,0,1:T(8,128)(2,1)}), bf16[1,64,32,128]{3,2,0,1:T(8,128)(2,1)S(1)}, u32[]{:S(2)}, u32[]{:S(2)}) async-start(bf16[1,64,32,128]{3,2,0,1:T(8,128)(2,1)} %get-tuple-element.48), calls=%async_computation | async-start | bytes 1048576 | tf_op jit(solution)/shard_map/all_to_all | solution.py:84
  113.3 17.1 %all-to-all-done = bf16[1,64,32,128]{3,2,0,1:T(8,128)(2,1)S(1)} async-done(((bf16[1,64,32,128]{3,2,0,1:T(8,128)(2,1)}), bf16[1,64,32,128]{3,2,0,1:T(8,128)(2,1)S(1)}, u32[]{:S(2)}, u32[]{:S(2)}) %all-to-all-start) | async-done | bytes 524320 | tf_op jit(solution)/shard_map/all_to_all | solution.py:84
  130.6 0.7 multiply_reduce_fusion
  131.2 9.8 %all-reduce.2 = (f32[]{:T(128)}, f32[]{:T(128)}) all-reduce(f32[]{:T(128)} %get-tuple-element.46, f32[]{:T(128)} %get-tuple-element.38), channel_id=1, replica_groups=mesh['wide_0'=4,'wide_1'=4,'wide_2'=2,'shard_0'=2,'shard_1'=4] {'wide_0'}, use_global_device_ids=true, to_apply=%region_3.5 | all-reduce | flops 2 | bytes 16 | tf_op jit(solution)/shard_map/psum | solution.py:22
  141.1 7.8 %all-reduce.1 = (f32[]{:T(128)}, f32[]{:T(128)}) all-reduce(f32[]{:T(128)} %get-tuple-element.32, f32[]{:T(128)} %get-tuple-element.33), channel_id=1, replica_groups=mesh['wide_0'=4,'wide_1'=4,'wide_2'=2,'shard_0'=2,'shard_1'=4] {'wide_1'}, use_global_device_ids=true, to_apply=%region_4.6 | all-reduce | flops 2 | bytes 16 | tf_op jit(solution)/shard_map/psum | solution.py:22
  148.9 6.8 %all-reduce.4 = (f32[]{:T(128)}, f32[]{:T(128)}) all-reduce(f32[]{:T(128)} %get-tuple-element.30, f32[]{:T(128)} %get-tuple-element.31), channel_id=1, replica_groups=mesh['wide_0'=4,'wide_1'=4,'wide_2'=2,'shard_0'=2,'shard_1'=4] {'wide_2'}, use_global_device_ids=true, to_apply=%region_5.7 | all-reduce | flops 2 | bytes 16 | tf_op jit(solution)/shard_map/psum | solution.py:22
  155.7 4.4 %all-reduce.3 = (f32[]{:T(128)}, f32[]{:T(128)}) all-reduce(f32[]{:T(128)} %get-tuple-element.36, f32[]{:T(128)} %get-tuple-element.37), channel_id=1, replica_groups=mesh['wide_0'=4,'wide_1'=4,'wide_2'=2,'shard_0'=2,'shard_1'=4] {'shard_0'}, use_global_device_ids=true, to_apply=%region_6.8 | all-reduce | flops 2 | bytes 16 | tf_op jit(solution)/shard_map/psum | solution.py:22
  160.1 9.1 %all-reduce = (f32[]{:T(128)}, f32[]{:T(128)}) all-reduce(f32[]{:T(128)} %get-tuple-element.34, f32[]{:T(128)} %get-tuple-element.35), channel_id=1, replica_groups=mesh['wide_0'=4,'wide_1'=4,'wide_2'=2,'shard_0'=2,'shard_1'=4] {'shard_1'}, use_global_device_ids=true, to_apply=%region_7.9 | all-reduce | flops 2 | bytes 16 | tf_op jit(solution)/shard_map/psum | solution.py:22
  169.9 0.9 broadcast_in_dim.50
  170.8 7.6 %all-to-all-start.3 = ((bf16[32,1,2,32,128]{4,3,2,1,0:T(8,128)(2,1)}), bf16[32,1,2,32,128]{4,3,2,1,0:T(8,128)(2,1)S(1)}, u32[]{:S(2)}, u32[]{:S(2)}) async-start(bf16[32,1,2,32,128]{4,3,2,1,0:T(8,128)(2,1)} %broadcast_in_dim.50), calls=%async_computation.3 | async-start | bytes 1048576 | tf_op jit(solution)/shard_map/all_to_all | solution.py:33
  178.4 2.2 fusion.22
  181.3 14.0 %all-to-all-done.3 = bf16[32,1,2,32,128]{4,3,2,1,0:T(8,128)(2,1)S(1)} async-done(((bf16[32,1,2,32,128]{4,3,2,1,0:T(8,128)(2,1)}), bf16[32,1,2,32,128]{4,3,2,1,0:T(8,128)(2,1)S(1)}, u32[]{:S(2)}, u32[]{:S(2)}) %all-to-all-start.3) | async-done | bytes 524320 | tf_op jit(solution)/shard_map/all_to_all | solution.py:33
  195.3 1.0 broadcast_in_dim.47
  196.2 5.8 %all-to-all-start.1 = ((bf16[32,1,2,32,128]{4,3,2,1,0:T(8,128)(2,1)}), bf16[32,1,2,32,128]{4,3,2,1,0:T(8,128)(2,1)}, u32[]{:S(2)}, u32[]{:S(2)}) async-start(bf16[32,1,2,32,128]{4,3,2,1,0:T(8,128)(2,1)} %broadcast_in_dim.47), calls=%async_computation.1 | async-start | bytes 1048576 | tf_op jit(solution)/shard_map/all_to_all | solution.py:33
  202.1 8.7 %fusion = bf16[1,128,64,128]{1,3,2,0:T(8,128)(2,1)S(1)} fusion(f32[1,128,64,128]{1,3,2,0:T(8,128)} %copy-done, f32[64,32,128]{2,1,0:T(8,128)} %fusion.22, f32[64,32,128]{2,1,0:T(8,128)S(1)} %bitcast.184), kind=kOutput, calls=%fused_computation.6 | convolution fusion | flops 404750336 | bytes 8388608 | tf_op jit(solution)/shard_map/rjpa,rjpb->rajb/dot_general | solution.py:57
  210.8 2.9 %copy.46 = bf16[1,128,8192]{2,1,0:T(8,128)(2,1)} copy(bf16[1,128,8192]{1,2,0:T(8,128)(2,1)S(1)} %bitcast.194) | data formatting | bytes 4194304
  213.7 4.3 %copy.35 = f32[128,8192]{0,1:T(8,128)} copy(bf16[128,8192]{1,0:T(8,128)(2,1)} %param.9) | data formatting | bytes 6291456 | tf_op jit(solution)/shard_map/reshape | solution.py:71
  218.1 0.6 pad_maximum_fusion
  218.8 0.6 gather_fusion.4
  219.5 1.2 bitcast_convert_fusion.1
  220.6 1.6 gather_fusion.2
  222.2 1.2 fusion.8
  223.5 2.6 %fusion.11 = f32[64,32,128]{2,1,0:T(8,128)S(1)} fusion(f32[64,32,128]{2,1,0:T(8,128)} %gather_fusion.2, pred[64]{0:T(512)(128)(4,1)S(1)} %and_bitcast_fusion, f32[128]{0:T(128)S(1)} %get-tuple-element.49, f32[128]{0:T(128)S(1)} %get-tuple-element.50), kind=kOutput, calls=%fused_computation.28 | convolution fusion | flops 402964480 | bytes 2098240 | tf_op jit(solution)/shard_map/rjpc,cb->rjpb/dot_general | solution.py:56
  226.1 6.7 %fusion.62 = f32[64,128,128]{2,1,0:T(8,128)S(1)} fusion(f32[64,32,128]{2,1,0:T(8,128)S(1)} %fusion.11, f32[64,32,128]{2,1,0:T(8,128)S(1)} %bitcast.185), kind=kOutput, calls=%fused_computation.105 | convolution fusion | flops 402653184 | bytes 6291456 | tf_op jit(solution)/shard_map/rjpa,rjpb->rajb/dot_general | solution.py:57
  232.8 7.4 %fusion.1 = bf16[1,128,64,128]{1,3,2,0:T(8,128)(2,1)S(1)} fusion(f32[1,128,64,128]{1,3,2,0:T(8,128)S(1)} %bitcast.187, f32[64,128,128]{2,1,0:T(8,128)S(1)} %fusion.62, f32[64,32,128]{2,1,0:T(8,128)S(1)} %fusion.8, f32[64,32,128]{2,1,0:T(8,128)S(1)} %bitcast.186), kind=kOutput, calls=%fused_computation.8 | convolution fusion | flops 407896064 | bytes 12582912 | tf_op jit(solution)/shard_map/rjpa,rjpb->rajb/dot_general | solution.py:57
  240.2 2.9 %copy.45 = bf16[128,8192]{1,0:T(8,128)(2,1)} copy(bf16[128,8192]{0,1:T(8,128)(2,1)S(1)} %bitcast.193) | data formatting | bytes 4194304
  (37 shorter events, 0.7 us)
Async XLA Ops:
  10.0 2.7 %copy-start.2 = (bf16[1,128,8192]{2,1,0:T(8,128)(2,1)S(1)}, bf16[1,128,8192]{2,1,0:T(8,128)(2,1)}, u32[]{:S(2)}) copy-start(bf16[1,128,8192]{2,1,0:T(8,128)(2,1)} %param.10) | copy-start | bytes 6291460
  66.2 7.9 %copy-start = (f32[1,128,64,128]{1,3,2,0:T(8,128)}, f32[1,128,64,128]{1,3,2,0:T(8,128)S(1)}, u32[]{:S(2)}) copy-start(f32[1,128,64,128]{1,3,2,0:T(8,128)S(1)} %fusion.3) | copy-start | bytes 12582916
  74.1 56.4 %copy-start.5 = (f32[1,2,32,128]{3,2,1,0:T(8,128)S(1)}, f32[1,2,32,128]{3,2,1,0:T(8,128)}, u32[]{:S(2)}) copy-start(f32[1,2,32,128]{3,2,1,0:T(8,128)} %param.15) | copy-start | bytes 98308
  74.1 56.4 %copy-start.6 = (f32[1,2,32,128]{3,2,1,0:T(8,128)S(1)}, f32[1,2,32,128]{3,2,1,0:T(8,128)}, u32[]{:S(2)}) copy-start(f32[1,2,32,128]{3,2,1,0:T(8,128)} %param.14) | copy-start | bytes 98308
  109.0 21.4 %all-to-all-start = ((bf16[1,64,32,128]{3,2,0,1:T(8,128)(2,1)}), bf16[1,64,32,128]{3,2,0,1:T(8,128)(2,1)S(1)}, u32[]{:S(2)}, u32[]{:S(2)}) async-start(bf16[1,64,32,128]{3,2,0,1:T(8,128)(2,1)} %get-tuple-element.48), calls=%async_computation | async-start | bytes 1048576 | tf_op jit(solution)/shard_map/all_to_all | solution.py:84
  131.2 79.6 %copy-start.7 = (f32[1,2,32,128]{3,2,1,0:T(8,128)}, f32[1,2,32,128]{3,2,1,0:T(8,128)S(1)}, u32[]{:S(2)}) copy-start(f32[1,2,32,128]{3,2,1,0:T(8,128)S(1)} %get-tuple-element.39) | copy-start | bytes 98308
  131.2 79.6 %copy-start.8 = (f32[1,2,32,128]{3,2,1,0:T(8,128)}, f32[1,2,32,128]{3,2,1,0:T(8,128)S(1)}, u32[]{:S(2)}) copy-start(f32[1,2,32,128]{3,2,1,0:T(8,128)S(1)} %get-tuple-element.40) | copy-start | bytes 98308
  170.8 24.5 %all-to-all-start.3 = ((bf16[32,1,2,32,128]{4,3,2,1,0:T(8,128)(2,1)}), bf16[32,1,2,32,128]{4,3,2,1,0:T(8,128)(2,1)S(1)}, u32[]{:S(2)}, u32[]{:S(2)}) async-start(bf16[32,1,2,32,128]{4,3,2,1,0:T(8,128)(2,1)} %broadcast_in_dim.50), calls=%async_computation.3 | async-start | bytes 1048576 | tf_op jit(solution)/shard_map/all_to_all | solution.py:33
  195.3 1.0 copy-start.3
  196.2 23.2 %all-to-all-start.1 = ((bf16[32,1,2,32,128]{4,3,2,1,0:T(8,128)(2,1)}), bf16[32,1,2,32,128]{4,3,2,1,0:T(8,128)(2,1)}, u32[]{:S(2)}, u32[]{:S(2)}) async-start(bf16[32,1,2,32,128]{4,3,2,1,0:T(8,128)(2,1)} %broadcast_in_dim.47), calls=%async_computation.1 | async-start | bytes 1048576 | tf_op jit(solution)/shard_map/all_to_all | solution.py:33
  213.7 4.4 %copy-start.9 = (s32[1,64]{1,0:T(1,128)S(1)}, s32[1,64]{1,0:T(1,128)}, u32[]{:S(2)}) copy-start(s32[1,64]{1,0:T(1,128)} %param.13) | copy-start | bytes 772
  213.7 5.0 %copy-start.4 = (bf16[32,1,2,32,128]{4,3,2,1,0:T(8,128)(2,1)S(1)}, bf16[32,1,2,32,128]{4,3,2,1,0:T(8,128)(2,1)}, u32[]{:S(2)}) copy-start(bf16[32,1,2,32,128]{4,3,2,1,0:T(8,128)(2,1)} %copy-done.3) | copy-start | bytes 1572868
  223.5 9.3 %copy-start.1 = (f32[128,8192]{0,1:T(8,128)S(1)}, f32[128,8192]{0,1:T(8,128)}, u32[]{:S(2)}) copy-start(f32[128,8192]{0,1:T(8,128)} %copy.35) | copy-start | bytes 12582916
where the time goes:
time: 248 us; the launch traced here: 244 us
  blocking collectives  68.6 us (28%)
  matrix products  61.9 us (25%)
  local copies, waits for them, and re-layouts  45.3 us (18%)
  waiting for transfers between devices  31.1 us (13%)
  starting transfers between devices  17.7 us (7%)
  other arithmetic  16.3 us (7%)
  between operations  2.73 us (1%)
    psum x5, blocking collectives, one_axis_at_a_time(): return functools.reduce(lax.psum, axes, shard)  37.9 us
    dot_general x4, matrix products, inverse(): return jnp.einsum('rjpa,rjpb->rajb', picked, right_part, precision=highest)  32.9 us
    all_to_all x1, blocking collectives, per_device(): lax.all_to_all(slot_band.astype(jnp.bfloat16), WIDE, split_axis=1, concat...  30.7 us
    dot_general x2, matrix products, per_device(): jnp.einsum('rjpa,rajb->rjpb', picked, blended, precision=highest)  19.4 us
    all_to_all x1, waiting for transfers between devices, per_device(): lax.all_to_all(slot_band.astype(jnp.bfloat16), WIDE, split_axis=1, concat...  17.1 us
    all_to_all x2, waiting for transfers between devices, from_everyone(): lax.all_to_all(jnp.broadcast_to(shard[None], (length, *shard.shape)), axi...  14 us
    all_to_all x2, starting transfers between devices, from_everyone(): lax.all_to_all(jnp.broadcast_to(shard[None], (length, *shard.shape)), axi...  13.4 us
    unnamed x25, local copies, waits for them, and re-layouts  11.9 us
  transfers between devices with their start and end apart: 3, of which 2 were waited for; matrix products, arithmetic and copies ran while one was open for 8% of the time, Pallas kernels for 0%

commit v1 on v0

--- a/solution.py
+++ b/solution.py
@@ -81,8 +81,14 @@
         band_coef = jnp.einsum("rjpb,cb->rjpc", left_part, basis, precision=highest)
         moment_now = blended - inverse(band_coef, picked, basis)
         slot_band = jnp.take_along_axis(band_coef, slot_order[:, :, None, None], axis=1)
-        pieces = lax.all_to_all(
-            slot_band.astype(jnp.bfloat16), WIDE, split_axis=1, concat_axis=0, tiled=True
+        pieces = jnp.concatenate(
+            lax.all_to_all(
+                jnp.stack(jnp.split(slot_band.astype(jnp.bfloat16), lax.axis_size(WIDE), axis=1)),
+                WIDE,
+                0,
+                0,
+            ),
+            axis=0,
         ).astype(slot_band.dtype)
         summed = jnp.sum(pieces.reshape((replicas, row_blocks) + pieces.shape[1:]), axis=0)
         mean_band = summed / replicas

time: 248 us -> 276 us (1.11)
  local copies, waits for them, and re-layouts: 45.3 us -> 84.3 us
  blocking collectives: 68.6 us -> 37.2 us
  starting transfers between devices: 17.7 us -> 36.3 us
    unnamed x25 -> x87, local copies, waits for them, and re-layouts: 11.9 us -> 49.5 us
    all_to_all x1 -> x0, blocking collectives: 30.7 us -> none  [per_device(): lax.all_to_all(slot_band.astype(jnp.bfloat16), WIDE, split_axis=1, concat...]
    all_to_all x1 -> x2, starting transfers between devices: 4.24 us -> 22.5 us  [per_device(): lax.all_to_all(jnp.stack(jnp.split(slot_band.astype(jnp.bfloat16), lax.ax...]
    all_to_all x1 -> x2, waiting for transfers between devices: 17.1 us -> 18.1 us  [per_device(): lax.all_to_all(jnp.stack(jnp.split(slot_band.astype(jnp.bfloat16), lax.ax...]
  transfers between devices with their start and end apart: 3 -> 4, of which waited for: 2 -> 3; matrix products, arithmetic and copies ran while one was open for 8% -> 14% of each run, Pallas kernels for 0% -> 0%
where the time goes in v1:
time: 276 us; the launch traced here: 272 us
  local copies, waits for them, and re-layouts  84.3 us (31%)
  matrix products  61.9 us (22%)
  blocking collectives  37.2 us (13%)
  starting transfers between devices  36.3 us (13%)
  waiting for transfers between devices  33.8 us (12%)
  other arithmetic  15.5 us (6%)
  between operations  2.84 us (1%)
    unnamed x87, local copies, waits for them, and re-layouts  49.5 us
    psum x5, blocking collectives, one_axis_at_a_time(): return functools.reduce(lax.psum, axes, shard)  37.2 us
    dot_general x4, matrix products, inverse(): return jnp.einsum('rjpa,rjpb->rajb', picked, right_part, precision=highest)  32.9 us
    all_to_all x2, starting transfers between devices, per_device(): lax.all_to_all(jnp.stack(jnp.split(slot_band.astype(jnp.bfloat16), lax.ax...  22.5 us
    dot_general x2, matrix products, per_device(): jnp.einsum('rjpa,rajb->rjpb', picked, blended, precision=highest)  19.4 us
    all_to_all x2, waiting for transfers between devices, per_device(): lax.all_to_all(jnp.stack(jnp.split(slot_band.astype(jnp.bfloat16), lax.ax...  18.1 us
    all_to_all x2, waiting for transfers between devices, from_everyone(): lax.all_to_all(jnp.broadcast_to(shard[None], (length, *shard.shape)), axi...  15.8 us
    all_to_all x2, starting transfers between devices, from_everyone(): lax.all_to_all(jnp.broadcast_to(shard[None], (length, *shard.shape)), axi...  13.8 us
  transfers between devices with their start and end apart: 4, of which 3 were waited for; matrix products, arithmetic and copies ran while one was open for 14% of the time, Pallas kernels for 0%

profile of v1, /device:TPU:1, one launch (start us, length us, event | category | flops | bytes accessed | tf_op | source)
XLA Modules:
  0.0 271.9 jit_solution(11202984502190465715)
XLA Ops:
  0.6 0.7 copy.26
  1.4 1.0 sort.17
  2.6 0.7 compare_select_fusion
  3.4 6.6 %slice_convert_fusion.1 = (f32[1,1,128,8192]{3,2,1,0:T(8,128)}, f32[16,8,64,128]{3,1,2,0:T(8,128)S(1)}, f32[1,1,128,8192]{3,2,1,0:T(8,128)}) fusion(bf16[2,1,128,8192]{3,2,1,0:T(8,128)(2,1)} %param.11), kind=kLoop, calls=%fused_computation.20 | loop fusion | flops 2097152 | bytes 16777216 | tf_op jit(solution)/shard_map/convert_element_type | solution.py:77
  10.0 2.7 copy.37
  12.7 2.5 convert_multiply_fusion
  15.3 2.7 copy.36
  18.2 6.0 %gather_fusion = f32[2048,128]{1,0:T(8,128)S(1)} fusion(f32[128,128]{1,0:T(8,128)S(1)} %cosine_multiply_fusion, s32[2048]{0:T(1024)S(1)} %broadcast_clamp_fusion), kind=kCustom, calls=%fused_computation.4 | custom fusion | bytes 2105344 | tf_op jit(solution)/shard_map/gather | solution.py:52
  24.2 12.7 %fusion.6 = f32[64,32,128]{2,1,0:T(8,128)S(1)} fusion(f32[64,32,128]{2,1,0:T(8,128)S(1)} %bitcast.425, f32[128,64,128]{2,1,0:T(8,128)} %bitcast.432, f32[128,64,128]{2,1,0:T(8,128)} %bitcast.433), kind=kOutput, calls=%fused_computation.16 | convolution fusion | flops 403701760 | bytes 10485760 | tf_op jit(solution)/shard_map/rjpa,rajb->rjpb/dot_general | solution.py:80
  36.9 1.2 fusion.28
  38.1 1.2 fusion.25
  39.3 5.6 %copy.30 = f32[1,1,128,8192]{2,3,1,0:T(8,128)} copy(f32[1,1,128,8192]{3,2,1,0:T(8,128)} %get-tuple-element.36) | data formatting | bytes 8388608 | tf_op jit(solution)/shard_map/convert_element_type | solution.py:77
  44.9 5.6 %copy.31 = f32[1,1,128,8192]{2,3,1,0:T(8,128)} copy(f32[1,1,128,8192]{3,2,1,0:T(8,128)} %get-tuple-element.38) | data formatting | bytes 8388608 | tf_op jit(solution)/shard_map/convert_element_type | solution.py:77
  50.5 5.6 %copy.29 = f32[1,128,8192]{1,2,0:T(8,128)} copy(f32[1,128,8192]{2,1,0:T(8,128)} %get-tuple-element.39) | data formatting | bytes 8388608 | tf_op jit(solution)/shard_map/mul | solution.py:77
  56.1 10.1 %fusion.3 = f32[1,128,64,128]{1,3,2,0:T(8,128)S(1)} fusion(f32[1,128,64,128]{1,3,2,0:T(8,128)} %bitcast.435, f32[1,128,64,128]{1,3,2,0:T(8,128)} %bitcast.436, f32[1,128,64,128]{1,3,2,0:T(8,128)} %bitcast.434, f32[64,32,128]{2,1,0:T(8,128)S(1)} %fusion.25, f32[64,32,128]{2,1,0:T(8,128)S(1)} %bitcast.426), kind=kOutput, calls=%fused_computation.11 | convolution fusion | flops 406847488 | bytes 18874368 | tf_op jit(solution)/shard_map/rjpa,rjpb->rajb/dot_general | solution.py:57
  66.2 6.7 %fusion.4 = f32[64,32,128]{2,1,0:T(8,128)S(1)} fusion(f32[64,32,128]{2,1,0:T(8,128)S(1)} %bitcast.427, f32[1,128,64,128]{1,3,2,0:T(8,128)S(1)} %fusion.3), kind=kOutput, calls=%fused_computation.13 | convolution fusion | flops 402653184 | bytes 6291456 | tf_op jit(solution)/shard_map/rjpa,rajb->rjpb/dot_general | solution.py:80
  72.8 1.2 fusion.23
  74.1 1.4 gather_fusion.1
  75.5 0.7 gather_fusion.3
  76.2 1.3 fusion.10
  77.5 0.6 constant_dynamic-update-slice_fusion.31
  96.9 12.7 %all-to-all-start = ((bf16[32,1,2,32,128]{4,3,2,1,0:T(8,128)(2,1)}), bf16[32,1,2,32,128]{4,3,2,1,0:T(8,128)(2,1)S(1)}, u32[]{:S(2)}, u32[]{:S(2)}) async-start(bf16[32,1,2,32,128]{4,3,2,1,0:T(8,128)(2,1)} %constant_dynamic-update-slice_fusion), calls=%async_computation | async-start | bytes 1048576 | tf_op jit(solution)/shard_map/all_to_all | solution.py:85
  109.7 0.6 constant_dynamic-update-slice_fusion.63
  129.1 9.8 %all-to-all-start.2 = ((bf16[32,1,2,32,128]{4,3,2,1,0:T(8,128)(2,1)}), bf16[32,1,2,32,128]{4,3,2,1,0:T(8,128)(2,1)S(1)}, u32[]{:S(2)}, u32[]{:S(2)}) async-start(bf16[32,1,2,32,128]{4,3,2,1,0:T(8,128)(2,1)} %constant_dynamic-update-slice_fusion.32), calls=%async_computation.2 | async-start | bytes 1048576 | tf_op jit(solution)/shard_map/all_to_all | solution.py:85
  139.0 18.1 %all-to-all-done.2 = bf16[32,1,2,32,128]{4,3,2,1,0:T(8,128)(2,1)S(1)} async-done(((bf16[32,1,2,32,128]{4,3,2,1,0:T(8,128)(2,1)}), bf16[32,1,2,32,128]{4,3,2,1,0:T(8,128)(2,1)S(1)}, u32[]{:S(2)}, u32[]{:S(2)}) %all-to-all-start.2) | async-done | bytes 524320 | tf_op jit(solution)/shard_map/all_to_all | solution.py:85
  157.2 0.7 multiply_reduce_fusion
  157.8 9.0 %all-reduce.2 = (f32[]{:T(128)}, f32[]{:T(128)}) all-reduce(f32[]{:T(128)} %get-tuple-element.41, f32[]{:T(128)} %get-tuple-element.33), channel_id=1, replica_groups=mesh['wide_0'=4,'wide_1'=4,'wide_2'=2,'shard_0'=2,'shard_1'=4] {'wide_0'}, use_global_device_ids=true, to_apply=%region_3.5 | all-reduce | flops 2 | bytes 16 | tf_op jit(solution)/shard_map/psum | solution.py:22
  166.8 8.0 %all-reduce.1 = (f32[]{:T(128)}, f32[]{:T(128)}) all-reduce(f32[]{:T(128)} %get-tuple-element.27, f32[]{:T(128)} %get-tuple-element.28), channel_id=1, replica_groups=mesh['wide_0'=4,'wide_1'=4,'wide_2'=2,'shard_0'=2,'shard_1'=4] {'wide_1'}, use_global_device_ids=true, to_apply=%region_4.6 | all-reduce | flops 2 | bytes 16 | tf_op jit(solution)/shard_map/psum | solution.py:22
  174.8 6.6 %all-reduce.4 = (f32[]{:T(128)}, f32[]{:T(128)}) all-reduce(f32[]{:T(128)} %get-tuple-element.25, f32[]{:T(128)} %get-tuple-element.26), channel_id=1, replica_groups=mesh['wide_0'=4,'wide_1'=4,'wide_2'=2,'shard_0'=2,'shard_1'=4] {'wide_2'}, use_global_device_ids=true, to_apply=%region_5.7 | all-reduce | flops 2 | bytes 16 | tf_op jit(solution)/shard_map/psum | solution.py:22
  181.4 4.4 %all-reduce.3 = (f32[]{:T(128)}, f32[]{:T(128)}) all-reduce(f32[]{:T(128)} %get-tuple-element.31, f32[]{:T(128)} %get-tuple-element.32), channel_id=1, replica_groups=mesh['wide_0'=4,'wide_1'=4,'wide_2'=2,'shard_0'=2,'shard_1'=4] {'shard_0'}, use_global_device_ids=true, to_apply=%region_6.8 | all-reduce | flops 2 | bytes 16 | tf_op jit(solution)/shard_map/psum | solution.py:22
  185.8 9.2 %all-reduce = (f32[]{:T(128)}, f32[]{:T(128)}) all-reduce(f32[]{:T(128)} %get-tuple-element.29, f32[]{:T(128)} %get-tuple-element.30), channel_id=1, replica_groups=mesh['wide_0'=4,'wide_1'=4,'wide_2'=2,'shard_0'=2,'shard_1'=4] {'shard_1'}, use_global_device_ids=true, to_apply=%region_7.9 | all-reduce | flops 2 | bytes 16 | tf_op jit(solution)/shard_map/psum | solution.py:22
  195.8 0.9 broadcast_in_dim.50
  196.7 8.9 %all-to-all-start.3 = ((bf16[32,1,2,32,128]{4,3,2,1,0:T(8,128)(2,1)}), bf16[32,1,2,32,128]{4,3,2,1,0:T(8,128)(2,1)S(1)}, u32[]{:S(2)}, u32[]{:S(2)}) async-start(bf16[32,1,2,32,128]{4,3,2,1,0:T(8,128)(2,1)} %broadcast_in_dim.50), calls=%async_computation.3 | async-start | bytes 1048576 | tf_op jit(solution)/shard_map/all_to_all | solution.py:33
  205.6 2.2 fusion.20
  208.5 15.4 %all-to-all-done.3 = bf16[32,1,2,32,128]{4,3,2,1,0:T(8,128)(2,1)S(1)} async-done(((bf16[32,1,2,32,128]{4,3,2,1,0:T(8,128)(2,1)}), bf16[32,1,2,32,128]{4,3,2,1,0:T(8,128)(2,1)S(1)}, u32[]{:S(2)}, u32[]{:S(2)}) %all-to-all-start.3) | async-done | bytes 524320 | tf_op jit(solution)/shard_map/all_to_all | solution.py:33
  223.8 1.0 broadcast_in_dim.47
  224.8 4.9 %all-to-all-start.1 = ((bf16[32,1,2,32,128]{4,3,2,1,0:T(8,128)(2,1)}), bf16[32,1,2,32,128]{4,3,2,1,0:T(8,128)(2,1)}, u32[]{:S(2)}, u32[]{:S(2)}) async-start(bf16[32,1,2,32,128]{4,3,2,1,0:T(8,128)(2,1)} %broadcast_in_dim.47), calls=%async_computation.1 | async-start | bytes 1048576 | tf_op jit(solution)/shard_map/all_to_all | solution.py:33
  229.7 8.7 %fusion = bf16[1,128,64,128]{1,3,2,0:T(8,128)(2,1)S(1)} fusion(f32[1,128,64,128]{1,3,2,0:T(8,128)} %copy-done, f32[64,32,128]{2,1,0:T(8,128)} %fusion.20, f32[64,32,128]{2,1,0:T(8,128)S(1)} %bitcast.428), kind=kOutput, calls=%fused_computation.6 | convolution fusion | flops 404750336 | bytes 8388608 | tf_op jit(solution)/shard_map/rjpa,rjpb->rajb/dot_general | solution.py:57
  238.4 2.9 %copy.34 = bf16[1,128,8192]{2,1,0:T(8,128)(2,1)} copy(bf16[1,128,8192]{1,2,0:T(8,128)(2,1)S(1)} %bitcast.438) | data formatting | bytes 4194304
  241.3 4.6 %copy.25 = f32[128,8192]{0,1:T(8,128)} copy(bf16[128,8192]{1,0:T(8,128)(2,1)} %param.9) | data formatting | bytes 6291456 | tf_op jit(solution)/shard_map/reshape | solution.py:71
  246.7 0.6 gather_fusion.4
  247.8 1.2 bitcast_convert_fusion.1
  248.9 1.6 gather_fusion.2
  250.5 1.2 fusion.8
  251.8 2.6 fusion.11
  254.4 6.7 %fusion.60 = f32[64,128,128]{2,1,0:T(8,128)S(1)} fusion(f32[64,32,128]{2,1,0:T(8,128)S(1)} %fusion.11, f32[64,32,128]{2,1,0:T(8,128)S(1)} %bitcast.429), kind=kOutput, calls=%fused_computation.231 | convolution fusion | flops 402653184 | bytes 6291456 | tf_op jit(solution)/shard_map/rjpa,rjpb->rajb/dot_general | solution.py:57
  261.1 7.4 %fusion.1 = bf16[1,128,64,128]{1,3,2,0:T(8,128)(2,1)S(1)} fusion(f32[1,128,64,128]{1,3,2,0:T(8,128)S(1)} %bitcast.431, f32[64,128,128]{2,1,0:T(8,128)S(1)} %fusion.60, f32[64,32,128]{2,1,0:T(8,128)S(1)} %fusion.8, f32[64,32,128]{2,1,0:T(8,128)S(1)} %bitcast.430), kind=kOutput, calls=%fused_computation.8 | convolution fusion | flops 407896064 | bytes 12582912 | tf_op jit(solution)/shard_map/rjpa,rjpb->rajb/dot_general | solution.py:57
  268.5 2.9 %copy.33 = bf16[128,8192]{1,0:T(8,128)(2,1)} copy(bf16[128,8192]{0,1:T(8,128)(2,1)S(1)} %bitcast.437) | data formatting | bytes 4194304
  (102 shorter events, 39.5 us)
Async XLA Ops:
  10.0 2.7 copy-start.2
  66.2 7.9 %copy-start = (f32[1,128,64,128]{1,3,2,0:T(8,128)}, f32[1,128,64,128]{1,3,2,0:T(8,128)S(1)}, u32[]{:S(2)}) copy-start(f32[1,128,64,128]{1,3,2,0:T(8,128)S(1)} %fusion.3) | copy-start | bytes 12582916
  75.5 81.6 %copy-start.5 = (f32[1,2,32,128]{3,2,1,0:T(8,128)S(1)}, f32[1,2,32,128]{3,2,1,0:T(8,128)}, u32[]{:S(2)}) copy-start(f32[1,2,32,128]{3,2,1,0:T(8,128)} %param.15) | copy-start | bytes 98308
  75.5 81.6 %copy-start.6 = (f32[1,2,32,128]{3,2,1,0:T(8,128)S(1)}, f32[1,2,32,128]{3,2,1,0:T(8,128)}, u32[]{:S(2)}) copy-start(f32[1,2,32,128]{3,2,1,0:T(8,128)} %param.14) | copy-start | bytes 98308
  96.9 32.2 %all-to-all-start = ((bf16[32,1,2,32,128]{4,3,2,1,0:T(8,128)(2,1)}), bf16[32,1,2,32,128]{4,3,2,1,0:T(8,128)(2,1)S(1)}, u32[]{:S(2)}, u32[]{:S(2)}) async-start(bf16[32,1,2,32,128]{4,3,2,1,0:T(8,128)(2,1)} %constant_dynamic-update-slice_fusion), calls=%async_computation | async-start | bytes 1048576 | tf_op jit(solution)/shard_map/all_to_all | solution.py:85
  129.1 27.9 %all-to-all-start.2 = ((bf16[32,1,2,32,128]{4,3,2,1,0:T(8,128)(2,1)}), bf16[32,1,2,32,128]{4,3,2,1,0:T(8,128)(2,1)S(1)}, u32[]{:S(2)}, u32[]{:S(2)}) async-start(bf16[32,1,2,32,128]{4,3,2,1,0:T(8,128)(2,1)} %constant_dynamic-update-slice_fusion.32), calls=%async_computation.2 | async-start | bytes 1048576 | tf_op jit(solution)/shard_map/all_to_all | solution.py:85
  157.8 80.6 %copy-start.7 = (f32[1,2,32,128]{3,2,1,0:T(8,128)}, f32[1,2,32,128]{3,2,1,0:T(8,128)S(1)}, u32[]{:S(2)}) copy-start(f32[1,2,32,128]{3,2,1,0:T(8,128)S(1)} %get-tuple-element.34) | copy-start | bytes 98308
  157.8 80.6 %copy-start.8 = (f32[1,2,32,128]{3,2,1,0:T(8,128)}, f32[1,2,32,128]{3,2,1,0:T(8,128)S(1)}, u32[]{:S(2)}) copy-start(f32[1,2,32,128]{3,2,1,0:T(8,128)S(1)} %get-tuple-element.35) | copy-start | bytes 98308
  196.7 27.2 %all-to-all-start.3 = ((bf16[32,1,2,32,128]{4,3,2,1,0:T(8,128)(2,1)}), bf16[32,1,2,32,128]{4,3,2,1,0:T(8,128)(2,1)S(1)}, u32[]{:S(2)}, u32[]{:S(2)}) async-start(bf16[32,1,2,32,128]{4,3,2,1,0:T(8,128)(2,1)} %broadcast_in_dim.50), calls=%async_computation.3 | async-start | bytes 1048576 | tf_op jit(solution)/shard_map/all_to_all | solution.py:33
  223.8 1.0 copy-start.3
  224.8 23.0 %all-to-all-start.1 = ((bf16[32,1,2,32,128]{4,3,2,1,0:T(8,128)(2,1)}), bf16[32,1,2,32,128]{4,3,2,1,0:T(8,128)(2,1)}, u32[]{:S(2)}, u32[]{:S(2)}) async-start(bf16[32,1,2,32,128]{4,3,2,1,0:T(8,128)(2,1)} %broadcast_in_dim.47), calls=%async_computation.1 | async-start | bytes 1048576 | tf_op jit(solution)/shard_map/all_to_all | solution.py:33
  241.3 4.6 %copy-start.9 = (s32[1,64]{1,0:T(1,128)S(1)}, s32[1,64]{1,0:T(1,128)}, u32[]{:S(2)}) copy-start(s32[1,64]{1,0:T(1,128)} %param.13) | copy-start | bytes 772
  241.3 5.2 %copy-start.4 = (bf16[32,1,2,32,128]{4,3,2,1,0:T(8,128)(2,1)S(1)}, bf16[32,1,2,32,128]{4,3,2,1,0:T(8,128)(2,1)}, u32[]{:S(2)}) copy-start(bf16[32,1,2,32,128]{4,3,2,1,0:T(8,128)(2,1)} %copy-done.3) | copy-start | bytes 1572868
  251.7 9.3 %copy-start.1 = (f32[128,8192]{0,1:T(8,128)S(1)}, f32[128,8192]{0,1:T(8,128)}, u32[]{:S(2)}) copy-start(f32[128,8192]{0,1:T(8,128)} %copy.25) | copy-start | bytes 12582916
